TPU v7x, 32 devices: a whole 2x2x4 slice. The times are simulated.
32 devices in a mesh: blk: 16 (over z, x, core), rep: 2 (over y).
Axes of the slice: x: 2, y: 2, z: 4, core: 2. Of those that a mesh axis runs over, the one named last changes fastest.
Arguments:
- prices: float32 [512], replicated, may hold values from 0.5 to 1.5
- capacity: float32 [512], replicated, may hold values from -8 to 8
- coupling: bfloat16 [48, 32, 512], P(None, 'blk', 'rep'), may hold values from -0.25 to 0.25
- assign: int32 [65536], P(('blk', 'rep')), may hold values from 0 to 31
- avail: int32 [48, 65536], P(None, ('blk', 'rep')), may hold values 0 or 1
- agent_cap: float32 [65536], P(('blk', 'rep')), may hold values from 0.5 to 2
- value: float32 [48, 65536], P(None, ('blk', 'rep')), may hold values from -6 to 6
- weight: float32 [48, 65536], P(None, ('blk', 'rep')), may hold values from 0.5 to 2
- warm: float32 [48, 65536], P(None, ('blk', 'rep')), may hold values from 0 to 2
Outputs:
- plan: float32 [48, 65536], P(None, ('blk', 'rep'))
- new_prices: float32 [512], replicated
All inputs are finite; a program needn't handle non-finite values. No bound on the sum of `avail` on one device may be relied on, other than what follows from the above.
Results may differ from a plain program's by a relative error of at most 0.0003.
Values may be sent and summed in bfloat16 or wider, within the bound.
A program may use at most 64 MiB of HBM per device.

v0:
```python
import jax
import jax.numpy as jnp
from jax import lax
from jax.sharding import PartitionSpec as P

INNER = 8


def smooth_of(plan_now):
    diffs = plan_now[1:] - plan_now[:-1]
    zero_row = jnp.zeros((1, plan_now.shape[1]), jnp.float32)
    return jnp.concatenate([zero_row, diffs], 0) - jnp.concatenate([diffs, zero_row], 0)


def price_block(slab_part, lam_half):
    return jnp.einsum(
        "tfr,r->tf", slab_part.astype(jnp.float32), lam_half, precision=lax.Precision.HIGHEST
    )


def sum_block(slab_part, load_part):
    return jnp.einsum(
        "tfr,tf->r", slab_part.astype(jnp.float32), load_part, precision=lax.Precision.HIGHEST
    )


def shards(prices, capacity, coupling, assign, avail, agent_cap, value, weight, warm):
    feed_local = coupling.shape[1]
    half_rows = coupling.shape[2]
    feeders = feed_local * lax.axis_size("blk")
    total_agents = warm.shape[1] * lax.axis_size("blk") * lax.axis_size("rep")
    row_start = lax.axis_index("rep") * half_rows
    lam_half = lax.dynamic_slice_in_dim(prices, row_start, half_rows, 0)
    onehot = (assign[None, :] == lax.iota(jnp.int32, feeders)[:, None]).astype(jnp.float32)
    half_table = price_block(lax.all_gather(coupling, "blk", axis=1, tiled=True), lam_half)
    table = lax.psum(half_table, "rep")
    price = jnp.dot(table, onehot, precision=lax.Precision.HIGHEST)
    upper = agent_cap[None, :] * avail.astype(jnp.float32)
    plan = jnp.clip(warm, 0.0, upper)
    for _ in range(INNER):
        gradient = weight * plan + 1.0 * smooth_of(plan) - value + price
        plan = jnp.clip(plan - 0.15 * gradient, 0.0, upper)
    local_loads = lax.dot_general(
        plan, onehot, (((1,), (1,)), ((), ())), precision=lax.Precision.HIGHEST
    )
    local_loads = local_loads * (feeders / total_agents)
    pair_loads = lax.psum(local_loads.astype(jnp.bfloat16), "rep").astype(jnp.float32)
    half_sums = sum_block(lax.all_gather(coupling, "blk", axis=1, tiled=True), pair_loads)
    placed = lax.dynamic_update_slice_in_dim(
        jnp.zeros(prices.shape, jnp.float32), half_sums, row_start, 0
    )
    sums = lax.psum(placed, ("blk", "rep"))
    new_prices = jnp.maximum(0.0, prices + 0.1 * (sums - capacity))
    return (plan, new_prices)


def solution(mesh):
    placed = (
        P(),
        P(),
        P(None, "blk", "rep"),
        P(("blk", "rep")),
        P(None, ("blk", "rep")),
        P(("blk", "rep")),
        P(None, ("blk", "rep")),
        P(None, ("blk", "rep")),
        P(None, ("blk", "rep")),
    )
    return jax.shard_map(
        shards,
        mesh=mesh,
        in_specs=placed,
        out_specs=(P(None, ("blk", "rep")), P()),
        check_vma=False,
    )
```

profile of v0, /device:TPU:14, one launch (start us, length us, event | category | flops | bytes accessed | tf_op | source)
XLA Modules:
  0.0 87.3 jit_solution(13477924110720840931)
XLA Ops:
  0.6 0.0 copy-start.7
  0.6 0.7 copy-done.7
  1.3 0.1 dynamic_slice.3
  1.4 0.8 copy.11
  2.2 17.3 %all_gather.4 = bf16[48,32,256]{2,0,1:T(8,128)(2,1)S(1)} all-gather(bf16[48,2,256]{2,0,1:T(8,128)(2,1)S(1)} %copy.11), channel_id=1, replica_groups=mesh['blk'=16,'rep'=2] {'blk'}, dimensions={1}, use_global_device_ids=true | all-gather | bytes 835584 | tf_op jit(solution)/shard_map/all_gather | solution.py:35
  19.5 0.0 copy-start
  19.5 0.0 copy-start.4
  19.5 1.2 %fusion.4 = f32[1,48,32]{1,0,2:T(1,128)S(1)} fusion(f32[256,1,1]{0,1,2:T(1,128)S(1)} %bitcast.12, bf16[48,32,256]{2,0,1:T(8,128)(2,1)S(1)} %all_gather.4), kind=kOutput, calls=%fused_computation.25 | convolution fusion | flops 4718592 | bytes 793600 | tf_op jit(solution)/shard_map/tfr,r->tf/dot_general | solution.py:16
  20.7 0.1 copy.12
  20.8 0.0 copy-start.5
  20.8 7.4 %psum.21 = f32[48,32]{1,0:T(8,128)S(1)} all-reduce(f32[48,32]{1,0:T(8,128)S(1)} %bitcast.10), channel_id=1, replica_groups=mesh['blk'=16,'rep'=2] {'rep'}, use_global_device_ids=true, to_apply=%region_0.0 | all-reduce | flops 1536 | bytes 12288 | tf_op jit(solution)/shard_map/psum | solution.py:36
  28.3 0.0 copy-done
  28.3 0.0 copy-done.4
  28.3 0.0 copy-done.5
  28.3 0.1 maximum_minimum_fusion.8
  28.4 0.0 copy-start.1
  28.4 0.0 copy-start.2
  28.4 0.0 copy-start.6
  28.4 0.9 %copy-done.1 = f32[48,2048]{1,0:T(8,128)S(1)} copy-done((f32[48,2048]{1,0:T(8,128)S(1)}, f32[48,2048]{1,0:T(8,128)}, u32[]{:S(2)}) %copy-start.1) | copy-done | bytes 393240
  29.4 0.1 copy-done.2
  29.5 0.0 copy-done.6
  29.5 0.5 maximum_minimum_fusion.7
  30.0 0.2 maximum_minimum_fusion.6
  30.3 0.3 maximum_minimum_fusion.5
  30.6 0.2 maximum_minimum_fusion.4
  30.9 0.3 maximum_minimum_fusion.3
  31.3 0.2 maximum_minimum_fusion.2
  31.5 0.3 maximum_minimum_fusion.1
  31.9 0.2 maximum_minimum_fusion
  32.1 0.0 copy-start.3
  32.1 0.3 fusion
  32.5 8.1 %psum.22 = bf16[48,32]{1,0:T(8,128)(2,1)S(1)} all-reduce(bf16[48,32]{1,0:T(8,128)(2,1)S(1)} %fusion), channel_id=1, replica_groups=mesh['blk'=16,'rep'=2] {'rep'}, use_global_device_ids=true, to_apply=%region_1.2 | all-reduce | flops 1536 | bytes 6144 | tf_op jit(solution)/shard_map/psum | solution.py:47
  40.6 0.1 copy.13
  40.7 0.3 fusion.5
  41.0 0.0 copy-done.3
  41.0 0.2 dynamic_update_slice.3
  41.2 0.0 copy-start.8
  41.2 45.5 %psum.23 = f32[512]{0:T(512)S(1)} all-reduce(f32[512]{0:T(512)S(1)} %dynamic_update_slice.3), channel_id=1, replica_groups=mesh['blk'=16,'rep'=2] {'blk','rep'}, use_global_device_ids=true, to_apply=%region_2.3 | all-reduce | flops 512 | bytes 4096 | tf_op jit(solution)/shard_map/psum | solution.py:52
  86.7 0.0 copy-done.8
  86.7 0.6 add_maximum_fusion
  (9 shorter events, 0.3 us)
Async XLA Ops:
  0.6 0.7 copy-start.7
  19.5 8.7 %copy-start = (s32[48,2048]{1,0:T(8,128)S(1)}, s32[48,2048]{1,0:T(8,128)}, u32[]{:S(2)}) copy-start(s32[48,2048]{1,0:T(8,128)} %param.13) | copy-start | bytes 1179652
  19.5 8.7 %copy-start.4 = (f32[48,2048]{1,0:T(8,128)S(1)}, f32[48,2048]{1,0:T(8,128)}, u32[]{:S(2)}) copy-start(f32[48,2048]{1,0:T(8,128)} %param.17) | copy-start | bytes 1179652
  20.8 7.5 %copy-start.5 = (f32[2048]{0:T(1024)S(1)}, f32[2048]{0:T(1024)}, u32[]{:S(2)}) copy-start(f32[2048]{0:T(1024)} %param.14) | copy-start | bytes 24580
  28.4 1.0 %copy-start.1 = (f32[48,2048]{1,0:T(8,128)S(1)}, f32[48,2048]{1,0:T(8,128)}, u32[]{:S(2)}) copy-start(f32[48,2048]{1,0:T(8,128)} %param.15) | copy-start | bytes 1179652
  28.4 1.1 %copy-start.2 = (f32[48,2048]{1,0:T(8,128)S(1)}, f32[48,2048]{1,0:T(8,128)}, u32[]{:S(2)}) copy-start(f32[48,2048]{1,0:T(8,128)} %param.16) | copy-start | bytes 1179652
  28.4 1.1 %copy-start.6 = (s32[2048]{0:T(1024)S(1)}, s32[2048]{0:T(1024)}, u32[]{:S(2)}) copy-start(s32[2048]{0:T(1024)} %param.12) | copy-start | bytes 24580
  32.1 8.8 %copy-start.3 = (f32[48,2048]{1,0:T(8,128)}, f32[48,2048]{1,0:T(8,128)S(1)}, u32[]{:S(2)}) copy-start(f32[48,2048]{1,0:T(8,128)S(1)} %maximum_minimum_fusion) | copy-start | bytes 1179652
  41.2 45.5 %copy-start.8 = (f32[512]{0:T(512)S(1)}, f32[512]{0:T(512)}, u32[]{:S(2)}) copy-start(f32[512]{0:T(512)} %param.10) | copy-start | bytes 6148
where the time goes:
time: 87.7 us; the launch traced here: 87.3 us
  blocking collectives  78.4 us (89%)
  local copies, waits for them, and re-layouts  3.02 us (3%)
  other arithmetic  2.8 us (3%)
  matrix products  2.29 us (3%)
    psum x1, blocking collectives, shards(): sums = lax.psum(placed, ('blk', 'rep'))  45.5 us
    all_gather x1, blocking collectives, shards(): lax.all_gather(coupling, 'blk', axis=1, tiled=True)  17.3 us
    psum x1, blocking collectives, shards(): lax.psum(local_loads.astype(jnp.bfloat16), 'rep').astype(jnp.float32)  8.11 us
    psum x1, blocking collectives, shards(): table = lax.psum(half_table, 'rep')  7.44 us
    unnamed x19, local copies, waits for them, and re-layouts  2.55 us
    min x7, other arithmetic, shards(): plan = jnp.clip(plan - 0.15 * gradient, 0.0, upper)  1.82 us

commit v1 on v0

--- a/solution.py
+++ b/solution.py
@@ -33,7 +33,7 @@
     lam_half = lax.dynamic_slice_in_dim(prices, row_start, half_rows, 0)
     onehot = (assign[None, :] == lax.iota(jnp.int32, feeders)[:, None]).astype(jnp.float32)
     half_table = price_block(lax.all_gather(coupling, "blk", axis=1, tiled=True), lam_half)
-    table = lax.psum(half_table, "rep")
+    table = jnp.sum(lax.all_gather(half_table, "rep"), axis=0)
     price = jnp.dot(table, onehot, precision=lax.Precision.HIGHEST)
     upper = agent_cap[None, :] * avail.astype(jnp.float32)
     plan = jnp.clip(warm, 0.0, upper)

time: 87.7 us -> 82.1 us (0.936)
  blocking collectives: 78.4 us -> 72.3 us
    psum x1 -> x0, blocking collectives: 7.44 us -> none  [shards(): table = lax.psum(half_table, 'rep')]
    all_gather x0 -> x1, blocking collectives: none -> 4.41 us  [shards(): table = jnp.sum(lax.all_gather(half_table, 'rep'), axis=0)]
    psum x1, blocking collectives: 8.11 us -> 5.02 us  [shards(): lax.psum(local_loads.astype(jnp.bfloat16), 'rep').astype(jnp.float32)]
where the time goes in v1:
time: 82.1 us; the launch traced here: 81.7 us
  blocking collectives  72.3 us (88%)
  local copies, waits for them, and re-layouts  3.52 us (4%)
  other arithmetic  2.8 us (3%)
  matrix products  2.34 us (3%)
    psum x1, blocking collectives, shards(): sums = lax.psum(placed, ('blk', 'rep'))  45.5 us
    all_gather x1, blocking collectives, shards(): lax.all_gather(coupling, 'blk', axis=1, tiled=True)  17.3 us
    psum x1, blocking collectives, shards(): lax.psum(local_loads.astype(jnp.bfloat16), 'rep').astype(jnp.float32)  5.02 us
    all_gather x1, blocking collectives, shards(): table = jnp.sum(lax.all_gather(half_table, 'rep'), axis=0)  4.41 us
    unnamed x19, local copies, waits for them, and re-layouts  3.21 us
    min x7, other arithmetic, shards(): plan = jnp.clip(plan - 0.15 * gradient, 0.0, upper)  1.82 us

profile of v1, /device:TPU:14, one launch (start us, length us, event | category | flops | bytes accessed | tf_op | source)
XLA Modules:
  0.0 81.7 jit_solution(5159544722315443330)
XLA Ops:
  0.6 0.0 copy-start.7
  0.6 0.7 copy-done.7
  1.3 0.1 dynamic_slice.3
  1.4 0.8 copy.12
  2.2 17.3 %all_gather.10 = bf16[48,32,256]{2,0,1:T(8,128)(2,1)S(1)} all-gather(bf16[48,2,256]{2,0,1:T(8,128)(2,1)S(1)} %copy.12), channel_id=1, replica_groups=mesh['blk'=16,'rep'=2] {'blk'}, dimensions={1}, use_global_device_ids=true | all-gather | bytes 835584 | tf_op jit(solution)/shard_map/all_gather | solution.py:35
  19.5 0.0 copy-start
  19.5 0.0 copy-start.4
  19.5 1.2 %fusion.6 = f32[1,48,32]{1,0,2:T(1,128)S(1)} fusion(f32[256,1,1]{0,1,2:T(1,128)S(1)} %bitcast.12, bf16[48,32,256]{2,0,1:T(8,128)(2,1)S(1)} %all_gather.10), kind=kOutput, calls=%fused_computation.27 | convolution fusion | flops 4718592 | bytes 793600 | tf_op jit(solution)/shard_map/tfr,r->tf/dot_general | solution.py:16
  20.7 4.4 %all-gather.1 = f32[2,48,32]{1,2,0:T(8,128)S(1)} all-gather(f32[1,48,32]{1,2,0:T(8,128)S(1)} %bitcast.10), channel_id=2, replica_groups=mesh['blk'=16,'rep'=2] {'rep'}, dimensions={0}, use_global_device_ids=true | all-gather | bytes 18432 | tf_op jit(solution)/shard_map/all_gather | solution.py:36
  25.2 0.0 copy-start.5
  25.2 0.0 copy-done
  25.2 0.0 copy-done.4
  25.2 0.7 copy-done.5
  25.9 0.1 maximum_minimum_fusion.8
  25.9 0.0 copy-start.1
  25.9 0.0 copy-start.2
  25.9 0.0 copy-start.6
  26.0 0.9 %copy-done.1 = f32[48,2048]{1,0:T(8,128)S(1)} copy-done((f32[48,2048]{1,0:T(8,128)S(1)}, f32[48,2048]{1,0:T(8,128)}, u32[]{:S(2)}) %copy-start.1) | copy-done | bytes 393240
  26.9 0.1 copy-done.2
  27.0 0.0 copy-done.6
  27.0 0.5 maximum_minimum_fusion.7
  27.6 0.2 maximum_minimum_fusion.6
  27.9 0.3 maximum_minimum_fusion.5
  28.3 0.2 maximum_minimum_fusion.4
  28.5 0.3 maximum_minimum_fusion.3
  28.9 0.2 maximum_minimum_fusion.2
  29.2 0.3 maximum_minimum_fusion.1
  29.5 0.2 maximum_minimum_fusion
  29.8 0.0 copy-start.3
  29.8 0.3 fusion
  30.1 5.0 %psum.14 = bf16[48,32]{0,1:T(8,128)(2,1)S(1)} all-reduce(bf16[48,32]{0,1:T(8,128)(2,1)S(1)} %fusion), channel_id=1, replica_groups=mesh['blk'=16,'rep'=2] {'rep'}, use_global_device_ids=true, to_apply=%region_1.2 | all-reduce | flops 1536 | bytes 6144 | tf_op jit(solution)/shard_map/psum | solution.py:47
  35.1 0.3 fusion.4
  35.4 0.0 copy-done.3
  35.4 0.2 dynamic_update_slice.3
  35.6 0.0 copy-start.8
  35.6 45.5 %psum.15 = f32[512]{0:T(512)S(1)} all-reduce(f32[512]{0:T(512)S(1)} %dynamic_update_slice.3), channel_id=1, replica_groups=mesh['blk'=16,'rep'=2] {'blk','rep'}, use_global_device_ids=true, to_apply=%region_2.3 | all-reduce | flops 512 | bytes 4096 | tf_op jit(solution)/shard_map/psum | solution.py:52
  81.2 0.0 copy-done.8
  81.2 0.6 add_maximum_fusion
  (10 shorter events, 0.3 us)
Async XLA Ops:
  0.6 0.7 copy-start.7
  19.5 5.6 %copy-start = (s32[48,2048]{1,0:T(8,128)S(1)}, s32[48,2048]{1,0:T(8,128)}, u32[]{:S(2)}) copy-start(s32[48,2048]{1,0:T(8,128)} %param.13) | copy-start | bytes 1179652
  19.5 5.7 %copy-start.4 = (f32[48,2048]{1,0:T(8,128)S(1)}, f32[48,2048]{1,0:T(8,128)}, u32[]{:S(2)}) copy-start(f32[48,2048]{1,0:T(8,128)} %param.17) | copy-start | bytes 1179652
  25.2 0.7 copy-start.5
  25.9 1.0 %copy-start.1 = (f32[48,2048]{1,0:T(8,128)S(1)}, f32[48,2048]{1,0:T(8,128)}, u32[]{:S(2)}) copy-start(f32[48,2048]{1,0:T(8,128)} %param.15) | copy-start | bytes 1179652
  25.9 1.1 %copy-start.2 = (f32[48,2048]{1,0:T(8,128)S(1)}, f32[48,2048]{1,0:T(8,128)}, u32[]{:S(2)}) copy-start(f32[48,2048]{1,0:T(8,128)} %param.16) | copy-start | bytes 1179652
  25.9 1.1 %copy-start.6 = (s32[2048]{0:T(1024)S(1)}, s32[2048]{0:T(1024)}, u32[]{:S(2)}) copy-start(s32[2048]{0:T(1024)} %param.12) | copy-start | bytes 24580
  29.8 5.7 %copy-start.3 = (f32[48,2048]{1,0:T(8,128)}, f32[48,2048]{1,0:T(8,128)S(1)}, u32[]{:S(2)}) copy-start(f32[48,2048]{1,0:T(8,128)S(1)} %maximum_minimum_fusion) | copy-start | bytes 1179652
  35.6 45.5 %copy-start.8 = (f32[512]{0:T(512)S(1)}, f32[512]{0:T(512)}, u32[]{:S(2)}) copy-start(f32[512]{0:T(512)} %param.10) | copy-start | bytes 6148

commit v2 on v0

--- a/solution.py
+++ b/solution.py
@@ -49,7 +49,7 @@
     placed = lax.dynamic_update_slice_in_dim(
         jnp.zeros(prices.shape, jnp.float32), half_sums, row_start, 0
     )
-    sums = lax.psum(placed, ("blk", "rep"))
+    sums = jnp.sum(lax.all_gather(placed, ("blk", "rep")), axis=0)
     new_prices = jnp.maximum(0.0, prices + 0.1 * (sums - capacity))
     return (plan, new_prices)
 

time: 87.7 us -> 116 us (1.32)
  the two profiles are of different devices: /device:TPU:14 before, /device:TPU:0 now
where the time goes in v2:
time: 116 us; the launch traced here: 115 us
  blocking collectives  106 us (91%)
  local copies, waits for them, and re-layouts  3.4 us (3%)
  other arithmetic  2.86 us (2%)
  matrix products  2.3 us (2%)
    all_gather x1, blocking collectives, shards(): sums = jnp.sum(lax.all_gather(placed, ('blk', 'rep')), axis=0)  65.1 us
    all_gather x1, blocking collectives, shards(): lax.all_gather(coupling, 'blk', axis=1, tiled=True)  25.4 us
    psum x1, blocking collectives, shards(): table = lax.psum(half_table, 'rep')  8.45 us
    psum x1, blocking collectives, shards(): lax.psum(local_loads.astype(jnp.bfloat16), 'rep').astype(jnp.float32)  7.09 us
    unnamed x20, local copies, waits for them, and re-layouts  3.16 us

profile of v2, /device:TPU:0, one launch (start us, length us, event | category | flops | bytes accessed | tf_op | source)
XLA Modules:
  0.0 115.5 jit_solution(5802998230608806676)
XLA Ops:
  0.6 0.0 copy-start.7
  0.6 0.7 copy-done.7
  1.3 0.1 dynamic_slice.3
  1.4 0.8 copy.11
  2.2 25.4 %all_gather.12 = bf16[48,32,256]{2,0,1:T(8,128)(2,1)S(1)} all-gather(bf16[48,2,256]{2,0,1:T(8,128)(2,1)S(1)} %copy.11), channel_id=1, replica_groups=mesh['blk'=16,'rep'=2] {'blk'}, dimensions={1}, use_global_device_ids=true | all-gather | bytes 835584 | tf_op jit(solution)/shard_map/all_gather | solution.py:35
  27.6 0.0 copy-start
  27.6 0.0 copy-start.4
  27.6 1.2 %fusion.5 = f32[1,48,32]{1,0,2:T(1,128)S(1)} fusion(f32[256,1,1]{0,1,2:T(1,128)S(1)} %bitcast.17, bf16[48,32,256]{2,0,1:T(8,128)(2,1)S(1)} %all_gather.12), kind=kOutput, calls=%fused_computation.27 | convolution fusion | flops 4718592 | bytes 793600 | tf_op jit(solution)/shard_map/tfr,r->tf/dot_general | solution.py:16
  28.8 0.1 copy.12
  28.9 0.0 copy-start.5
  28.9 8.5 %psum.14 = f32[48,32]{1,0:T(8,128)S(1)} all-reduce(f32[48,32]{1,0:T(8,128)S(1)} %bitcast.15), channel_id=1, replica_groups=mesh['blk'=16,'rep'=2] {'rep'}, use_global_device_ids=true, to_apply=%region_0.0 | all-reduce | flops 1536 | bytes 12288 | tf_op jit(solution)/shard_map/psum | solution.py:36
  37.4 0.0 copy-done
  37.4 0.0 copy-done.4
  37.4 0.0 copy-done.5
  37.4 0.1 maximum_minimum_fusion.8
  37.5 0.0 copy-start.1
  37.5 0.0 copy-start.2
  37.5 0.0 copy-start.6
  37.5 0.9 copy-done.1
  38.5 0.1 copy-done.2
  38.6 0.0 copy-done.6
  38.6 0.5 maximum_minimum_fusion.7
  39.1 0.2 maximum_minimum_fusion.6
  39.4 0.3 maximum_minimum_fusion.5
  39.8 0.2 maximum_minimum_fusion.4
  40.0 0.3 maximum_minimum_fusion.3
  40.4 0.2 maximum_minimum_fusion.2
  40.6 0.3 maximum_minimum_fusion.1
  41.0 0.2 maximum_minimum_fusion
  41.2 0.0 copy-start.3
  41.3 0.3 fusion
  41.6 7.1 %psum.15 = bf16[48,32]{1,0:T(8,128)(2,1)S(1)} all-reduce(bf16[48,32]{1,0:T(8,128)(2,1)S(1)} %fusion), channel_id=1, replica_groups=mesh['blk'=16,'rep'=2] {'rep'}, use_global_device_ids=true, to_apply=%region_1.2 | all-reduce | flops 1536 | bytes 6144 | tf_op jit(solution)/shard_map/psum | solution.py:47
  48.7 0.1 copy.13
  48.8 0.3 fusion.1
  49.1 0.0 copy-done.3
  49.1 65.1 %all-gather = f32[32,1,512]{2,1,0:T(1,128)S(1)} all-gather(f32[1,1,512]{2,1,0:T(1,128)S(1)} %fusion.1), channel_id=1, replica_groups=mesh['blk'=16,'rep'=2] {'blk','rep'}, dimensions={0}, use_global_device_ids=true | all-gather | bytes 67584 | tf_op jit(solution)/shard_map/all_gather | solution.py:52
  114.2 0.0 copy-start.8
  114.2 0.1 reduce_sum.9
  114.3 0.6 copy-done.8
  114.9 0.6 add_maximum_fusion
  (9 shorter events, 0.3 us)
Async XLA Ops:
  0.6 0.7 copy-start.7
  27.6 9.7 %copy-start = (s32[48,2048]{1,0:T(8,128)S(1)}, s32[48,2048]{1,0:T(8,128)}, u32[]{:S(2)}) copy-start(s32[48,2048]{1,0:T(8,128)} %param.13) | copy-start | bytes 1179652
  27.6 9.8 %copy-start.4 = (f32[48,2048]{1,0:T(8,128)S(1)}, f32[48,2048]{1,0:T(8,128)}, u32[]{:S(2)}) copy-start(f32[48,2048]{1,0:T(8,128)} %param.17) | copy-start | bytes 1179652
  28.9 8.5 %copy-start.5 = (f32[2048]{0:T(1024)S(1)}, f32[2048]{0:T(1024)}, u32[]{:S(2)}) copy-start(f32[2048]{0:T(1024)} %param.14) | copy-start | bytes 24580
  37.5 1.0 copy-start.1
  37.5 1.1 copy-start.2
  37.5 1.1 copy-start.6
  41.2 7.8 %copy-start.3 = (f32[48,2048]{1,0:T(8,128)}, f32[48,2048]{1,0:T(8,128)S(1)}, u32[]{:S(2)}) copy-start(f32[48,2048]{1,0:T(8,128)S(1)} %maximum_minimum_fusion) | copy-start | bytes 1179652
  114.2 0.7 copy-start.8
